TPU v7x, 16 devices: a 4x2x1 block of a 4x4x8 slice. The times are simulated.
16 devices in a mesh: rep: 4 (over y, z, core), dp: 4 (over x).
Axes of the slice: x: 4, y: 2, z: 1, core: 2. Of those that a mesh axis runs over, the one named last changes fastest.
The devices are a block of a 4x4x8 slice.
Arguments:
- x: bfloat16 [16, 4096, 512], P(('rep', 'dp')), parts along dimension 0
- dy: bfloat16 [16, 4096, 512], P(('rep', 'dp')), parts along dimension 0
- w_gate: bfloat16 [2, 512, 3072], replicated
- w_up: bfloat16 [2, 512, 3072], replicated
- w_down: bfloat16 [2, 3072, 512], replicated
- m_w_gate: float32 [2, 512, 3072], P(None, 'dp')
- m_w_up: float32 [2, 512, 3072], P(None, 'dp')
- m_w_down: float32 [2, 3072, 512], P(None, 'dp')
- v_w_gate: float32 [2, 512, 3072], P(None, 'dp')
- v_w_up: float32 [2, 512, 3072], P(None, 'dp')
- v_w_down: float32 [2, 3072, 512], P(None, 'dp')
Outputs:
- output 1: bfloat16 [8, 512, 3072], P('rep'), parts along dimension 0
- output 2: bfloat16 [8, 512, 3072], P('rep'), parts along dimension 0
- output 3: bfloat16 [8, 3072, 512], P('rep'), parts along dimension 0
- output 4: float32 [8, 512, 3072], P('rep', 'dp'), parts along dimension 0
- output 5: float32 [8, 512, 3072], P('rep', 'dp'), parts along dimension 0
- output 6: float32 [8, 3072, 512], P('rep', 'dp'), parts along dimension 0
- output 7: float32 [8, 512, 3072], P('rep', 'dp'), parts along dimension 0
- output 8: float32 [8, 512, 3072], P('rep', 'dp'), parts along dimension 0
- output 9: float32 [8, 3072, 512], P('rep', 'dp'), parts along dimension 0
There are 4 independent parts. A program takes and returns all parts, laid end to end along the dimension named above; an argument that names none is the same for every part.
All inputs are finite; a program needn't handle non-finite values.
Results may differ from a plain program's by a relative error of at most 0.022.
Values are sent between devices in bfloat16 or wider.
A program may use at most 768 MiB of HBM per device.

v0:
```python
import jax
import jax.numpy as jnp
from jax import lax

NAMES = ("w_gate", "w_up", "w_down")


def matmul(a, w):
    return jnp.dot(a, w, preferred_element_type=jnp.float32).astype(jnp.bfloat16)


def normed(h):
    wide = h.astype(jnp.float32)
    scale = lax.rsqrt(jnp.mean(wide**2, -1, keepdims=True) + 1e-6)
    return (wide * scale).astype(jnp.bfloat16)


def layer(h, w):
    a = normed(h)
    gate = jnp.dot(a, w["w_gate"], preferred_element_type=jnp.float32)
    up = jnp.dot(a, w["w_up"], preferred_element_type=jnp.float32)
    return h + matmul((jax.nn.silu(gate) * up).astype(jnp.bfloat16), w["w_down"])


def adamw(w, m, v, g):
    m = 0.9 * m + 0.1 * g
    v = 0.95 * v + 0.05 * g * g
    step = m * lax.rsqrt(v + 1e-8) + 0.1 * w
    return (w - 0.02 * step).astype(jnp.bfloat16), m, v


def stack(weights, h):
    for number in range(weights["w_gate"].shape[0]):
        h = layer(h, {name: w[number] for name, w in weights.items()})
    return h


def solution(mesh):
    groups = mesh.shape["rep"]

    def step(x, dy, *arrays):
        weights, m, v = (arrays[i : i + 3] for i in (0, 3, 6))
        x, dy = (t.reshape(groups, -1, *t.shape[1:]) for t in (x, dy))

        def of_a_group(x, dy):
            _, back = jax.vjp(lambda w: stack(w, x), dict(zip(NAMES, weights, strict=True)))
            by_weights = back(dy)[0]
            gradients = [by_weights[name].astype(jnp.float32) for name in NAMES]
            new = [adamw(w.astype(jnp.float32), m, v, g) for w, m, v, g in zip(weights, m, v, gradients, strict=True)]
            return tuple(one[which] for which in range(3) for one in new)

        return tuple(t.reshape(-1, *t.shape[2:]) for t in jax.vmap(of_a_group)(x, dy))

    return step
```

profile of v0, /device:TPU:112, one launch (start us, length us, event | category | flops | bytes accessed | tf_op | source)
XLA Modules:
  0.0 915.6 jit_solution(15788390041832628058)
XLA Ops:
  16.8 23.6 %fusion.106 = f32[4096,3072]{1,0:T(8,128)} fusion(bf16[2,512,3072]{2,1,0:T(8,128)(2,1)} %param, bf16[1,4096,512]{2,1,0:T(8,128)(2,1)} %param.2, f32[4096]{0:T(1024)S(1)} %add_rsqrt_fusion), kind=kOutput, calls=%fused_computation.124 | convolution fusion | flops 12891193344 | bytes 57688064 | tf_op jit(solution)/vmap(jvp())/dot_general | solution.py:20
  40.4 23.0 %fusion.104 = f32[4096,3072]{1,0:T(8,128)} fusion(bf16[2,512,3072]{2,1,0:T(8,128)(2,1)} %param.3, bf16[1,4096,512]{2,1,0:T(8,128)(2,1)S(1)} %copy-done, f32[4096]{0:T(1024)S(1)} %add_rsqrt_fusion), kind=kOutput, calls=%fused_computation.122 | convolution fusion | flops 12891193344 | bytes 57688064 | tf_op jit(solution)/vmap(jvp())/dot_general | solution.py:21
  63.5 40.4 %fusion.26 = bf16[4096,3072]{1,0:T(8,128)(2,1)} fusion(f32[4096,3072]{1,0:T(8,128)} %fusion.104, f32[4096,3072]{1,0:T(8,128)} %fusion.106), kind=kLoop, calls=%fused_computation.35 | loop fusion | flops 75497472 | bytes 125829120
  103.8 22.2 %fusion.39 = (f32[4096]{0:T(1024)S(1)}, bf16[1,1,4096,512]{2,3,1,0:T(8,128)(2,1)}) fusion(bf16[4096,3072]{1,0:T(8,128)(2,1)} %fusion.26, bf16[2,3072,512]{2,1,0:T(8,128)(2,1)} %param.4, bf16[1,4096,512]{1,2,0:T(8,128)(2,1)} %copy), kind=kOutput, calls=%fused_computation.56 | convolution fusion | flops 12895383552 | bytes 36716544 | tf_op jit(solution)/vmap(jvp())/dot_general | solution.py:9
  126.7 23.6 %fusion.95 = f32[4096,3072]{1,0:T(8,128)} fusion(bf16[2,512,3072]{2,1,0:T(8,128)(2,1)} %param, bf16[1,1,4096,512]{2,3,1,0:T(8,128)(2,1)} %get-tuple-element.10, f32[4096]{0:T(1024)S(1)} %bitcast.380), kind=kOutput, calls=%fused_computation.113 | convolution fusion | flops 12891193344 | bytes 57688064 | tf_op jit(solution)/vmap(jvp())/dot_general | solution.py:20
  150.2 21.8 %fusion.98 = f32[4096,3072]{1,0:T(8,128)} fusion(bf16[2,512,3072]{2,1,0:T(8,128)(2,1)} %param.3, bf16[1,1,4096,512]{2,3,1,0:T(8,128)(2,1)S(1)} %copy-done.2, f32[4096]{0:T(1024)S(1)} %bitcast.381), kind=kOutput, calls=%fused_computation.116 | convolution fusion | flops 12891193344 | bytes 57688064 | tf_op jit(solution)/vmap(jvp())/dot_general | solution.py:21
  172.0 20.8 %convolution_convert_fusion.1 = bf16[4096,3072]{1,0:T(8,128)(2,1)} fusion(bf16[1,4096,512]{2,1,0:T(8,128)(2,1)} %param.5, bf16[2,3072,512]{2,1,0:T(8,128)(2,1)} %param.4), kind=kOutput, calls=%fused_computation.44 | convolution fusion | flops 12897484800 | bytes 32505856 | tf_op jit(solution)/vmap(transpose(jvp()))/dot_general | solution.py:9
  199.3 48.6 %fusion.6 = bf16[4096,3072]{1,0:T(8,128)(2,1)} fusion(f32[4096,3072]{1,0:T(8,128)} %fusion.95, f32[4096,3072]{1,0:T(8,128)} %fusion.98, bf16[4096,3072]{1,0:T(8,128)(2,1)} %convolution_convert_fusion.1), kind=kLoop, calls=%fused_computation.11 | loop fusion | flops 150994944 | bytes 150994944
  247.9 19.3 %convolution_convert_fusion.2 = bf16[4096,512]{0,1:T(8,128)(2,1)} fusion(bf16[4096,3072]{1,0:T(8,128)(2,1)} %fusion.6, bf16[2,512,3072]{2,1,0:T(8,128)(2,1)S(1)} %bitcast.376), kind=kOutput, calls=%fused_computation.61 | convolution fusion | flops 12884901888 | bytes 32505856 | tf_op jit(solution)/vmap(transpose(jvp()))/dot_general | solution.py:20
  267.2 35.0 %fusion.41 = (f32[4096]{0:T(1024)S(1)}, bf16[1,1,4096,512]{2,3,1,0:T(8,128)(2,1)}) fusion(bf16[1,1,4096,512]{2,3,1,0:T(8,128)(2,1)} %get-tuple-element.10, bf16[4096,512]{0,1:T(8,128)(2,1)} %convolution_convert_fusion.2, bf16[2,512,3072]{2,1,0:T(8,128)(2,1)} %param.3, bf16[4096,3072]{1,0:T(8,128)(2,1)} %convolution_convert_fusion.1, f32[4096,3072]{1,0:T(8,128)} %fusion.95), kind=kOutput, calls=%fused_computation.58 | convolution fusion | flops 12972978176 | bytes 91242496 | tf_op jit(solution)/vmap(transpose(jvp()))/dot_general | solution.py:21
  310.7 18.5 %convolution_bitcast_fusion = f32[1,3072,512]{2,1,0:T(8,128)} fusion(bf16[4096,3072]{1,0:T(8,128)(2,1)} %fusion.26, bf16[4096,512]{0,1:T(8,128)(2,1)S(1)} %fusion.68), kind=kOutput, calls=%fused_computation.70 | convolution fusion | flops 12884901888 | bytes 35651584 | tf_op jit(solution)/vmap(transpose(jvp()))/dot_general | solution.py:9
  329.4 36.9 %fusion.53 = f32[1,3072,512]{2,1,0:T(8,128)} fusion(f32[4096,3072]{1,0:T(8,128)} %fusion.98, f32[4096,3072]{1,0:T(8,128)} %fusion.95, bf16[1,4096,512]{2,1,0:T(8,128)(2,1)} %param.5), kind=kOutput, calls=%fused_computation.67 | convolution fusion | flops 12960399360 | bytes 111149056 | tf_op jit(solution)/vmap(transpose(jvp()))/dot_general | solution.py:9
  366.4 21.0 %convolution_convert_fusion = bf16[4096,3072]{1,0:T(8,128)(2,1)} fusion(bf16[4096,512]{0,1:T(8,128)(2,1)} %copy-done.3, bf16[2,3072,512]{2,1,0:T(8,128)(2,1)} %param.4), kind=kOutput, calls=%fused_computation.43 | convolution fusion | flops 12897484800 | bytes 32505856 | tf_op jit(solution)/vmap(transpose(jvp()))/dot_general | solution.py:9
  387.5 30.6 %fusion.59 = f32[1,512,3072]{2,1,0:T(8,128)} fusion(bf16[4096,3072]{1,0:T(8,128)(2,1)} %convolution_convert_fusion, f32[4096,3072]{1,0:T(8,128)} %fusion.106, bf16[1,4096,512]{1,2,0:T(8,128)(2,1)} %copy, f32[4096]{0:T(1024)S(1)} %copy-done.10), kind=kOutput, calls=%fused_computation.69 | convolution fusion | flops 12966690816 | bytes 85999616 | tf_op jit(solution)/vmap(transpose(jvp()))/dot_general | solution.py:21
  418.8 30.8 %fusion.56 = f32[1,512,3072]{2,1,0:T(8,128)} fusion(bf16[4096,3072]{1,0:T(8,128)(2,1)} %convolution_convert_fusion.1, f32[4096,3072]{1,0:T(8,128)} %fusion.95, bf16[1,1,4096,512]{2,3,1,0:T(8,128)(2,1)} %get-tuple-element.10, f32[4096]{0:T(1024)S(1)} %bitcast.383), kind=kOutput, calls=%fused_computation.68 | convolution fusion | flops 12966690816 | bytes 85999616 | tf_op jit(solution)/vmap(transpose(jvp()))/dot_general | solution.py:21
  449.7 19.4 %convolution_bitcast_fusion.1 = f32[1,512,3072]{2,1,0:T(8,128)} fusion(bf16[4096,3072]{1,0:T(8,128)(2,1)} %fusion.6, bf16[1,1,4096,512]{2,3,1,0:T(8,128)(2,1)} %get-tuple-element.10, f32[4096]{0:T(1024)S(1)} %bitcast.384), kind=kOutput, calls=%fused_computation.71 | convolution fusion | flops 12891193344 | bytes 35667968 | tf_op jit(solution)/vmap(transpose(jvp()))/dot_general | solution.py:20
  469.2 48.0 %fusion.62 = f32[1,512,3072]{2,1,0:T(8,128)} fusion(f32[4096,3072]{1,0:T(8,128)} %fusion.106, f32[4096,3072]{1,0:T(8,128)} %fusion.104, bf16[4096,3072]{1,0:T(8,128)(2,1)} %convolution_convert_fusion, bf16[1,4096,512]{1,2,0:T(8,128)(2,1)} %copy, f32[4096]{0:T(1024)S(1)} %copy-done.10), kind=kOutput, calls=%fused_computation.72 | convolution fusion | flops 13029605376 | bytes 136331264 | tf_op jit(solution)/vmap(transpose(jvp()))/dot_general | solution.py:20
  530.0 48.4 %reduce-scatter.23.cloned.1.call-done = f32[1,128,3072]{2,1,0:T(8,128)} async-done(((f32[1,512,3072]{2,1,0:T(8,128)}), f32[1,128,3072]{2,1,0:T(8,128)}) %reduce-scatter.23.cloned.1.call-update) | async-done | bytes 1572880
  586.2 54.5 %reduce-scatter.19.cloned.1.call-done = f32[1,128,3072]{2,1,0:T(8,128)} async-done(((f32[1,512,3072]{2,1,0:T(8,128)}), f32[1,128,3072]{2,1,0:T(8,128)}) %reduce-scatter.19.cloned.1.call-update) | async-done | bytes 1572880
  642.3 60.8 %reduce-scatter.21.cloned.1.call-done = f32[1,128,3072]{2,1,0:T(8,128)} async-done(((f32[1,512,3072]{2,1,0:T(8,128)}), f32[1,128,3072]{2,1,0:T(8,128)}) %reduce-scatter.21.cloned.1.call-update) | async-done | bytes 1572880
  710.8 55.1 %all-gather.14.cloned.1.call-done = bf16[1,2,3072,512]{3,2,1,0:T(8,128)(2,1)} async-done(((bf16[1,2,768,512]{3,2,1,0:T(8,128)(2,1)}), bf16[1,2,3072,512]{3,2,1,0:T(8,128)(2,1)}) %all-gather.14.cloned.1.call-update) | async-done | bytes 6291472 | tf_op jit(solution)/reshape | solution.py:52
  766.0 64.4 %all-gather.12.cloned.1.call-done = bf16[1,2,512,3072]{3,2,1,0:T(8,128)(2,1)} async-done(((bf16[1,2,128,3072]{3,2,1,0:T(8,128)(2,1)}), bf16[1,2,512,3072]{3,2,1,0:T(8,128)(2,1)}) %all-gather.12.cloned.1.call-update) | async-done | bytes 6291472 | tf_op jit(solution)/reshape | solution.py:52
  830.4 64.4 %all-gather.10.cloned.1.call-done = bf16[1,2,512,3072]{3,2,1,0:T(8,128)(2,1)} async-done(((bf16[1,2,128,3072]{3,2,1,0:T(8,128)(2,1)}), bf16[1,2,512,3072]{3,2,1,0:T(8,128)(2,1)}) %all-gather.10.cloned.1.call-update) | async-done | bytes 6291472 | tf_op jit(solution)/reshape | solution.py:52
  894.8 6.6 copy.5
  (75 shorter events, 62.6 us)
Async XLA Ops:
  7.2 511.9 %reduce-scatter.29.cloned.1.call-start = ((), (), s32[]{:S(2)}) async-start(), calls=%async_computation.14 | async-start | bytes 7864320
  16.8 23.7 %copy-start.9 = (f32[4096]{0:T(1024)}, f32[4096]{0:T(1024)S(1)}, u32[]{:S(2)}) copy-start(f32[4096]{0:T(1024)S(1)} %add_rsqrt_fusion) | copy-start | bytes 49156
  16.8 23.7 %copy-start = (bf16[1,4096,512]{2,1,0:T(8,128)(2,1)S(1)}, bf16[1,4096,512]{2,1,0:T(8,128)(2,1)}, u32[]{:S(2)}) copy-start(bf16[1,4096,512]{2,1,0:T(8,128)(2,1)} %param.2) | copy-start | bytes 12582916
  126.1 24.1 %copy-start.6 = (f32[1,1,4096]{2,1,0:T(1,128)}, f32[1,1,4096]{2,1,0:T(1,128)S(1)}, u32[]{:S(2)}) copy-start(f32[1,1,4096]{2,1,0:T(1,128)S(1)} %rsqrt.31) | copy-start | bytes 49156
  126.7 23.6 %copy-start.2 = (bf16[1,1,4096,512]{2,3,1,0:T(8,128)(2,1)S(1)}, bf16[1,1,4096,512]{2,3,1,0:T(8,128)(2,1)}, u32[]{:S(2)}) copy-start(bf16[1,1,4096,512]{2,3,1,0:T(8,128)(2,1)} %get-tuple-element.10) | copy-start | bytes 12582916
  192.8 55.1 %slice-start.2 = ((s8[6291456]{0:T(1024)(128)(4,1)}), s8[2097152]{0:T(1024)(128)(4,1)S(1)}, s32[]{:S(2)}) async-start(s8[6291456]{0:T(1024)(128)(4,1)} %bitcast.375), calls=%async_computation.17 | async-start | bytes 4194304
  199.3 48.7 %slice-start.3 = ((s8[6291456]{0:T(1024)(128)(4,1)}), s8[4194304]{0:T(1024)(128)(4,1)S(1)}, s32[]{:S(2)}) async-start(s8[6291456]{0:T(1024)(128)(4,1)} %bitcast.375), calls=%async_computation.18 | async-start | bytes 8388608
  267.2 35.0 %copy-start.5 = (f32[4096]{0:T(1024)S(1)}, f32[4096]{0:T(1024)}, u32[]{:S(2)}) copy-start(f32[4096]{0:T(1024)} %copy-done.4) | copy-start | bytes 49156
  267.2 35.1 %copy-start.7 = (f32[1,1,4096]{2,1,0:T(1,128)S(1)}, f32[1,1,4096]{2,1,0:T(1,128)}, u32[]{:S(2)}) copy-start(f32[1,1,4096]{2,1,0:T(1,128)} %copy-done.6) | copy-start | bytes 49156
  308.7 2.0 copy-start.3
  329.3 191.4 %reduce-scatter.27.cloned.1.call-start = ((), (), s32[]{:S(2)}) async-start(), calls=%async_computation.13 | async-start | bytes 7864320
  366.3 21.1 %copy-start.10 = (f32[4096]{0:T(1024)S(1)}, f32[4096]{0:T(1024)}, u32[]{:S(2)}) copy-start(f32[4096]{0:T(1024)} %copy-done.9) | copy-start | bytes 49156
  366.4 162.1 %reduce-scatter.25.cloned.1.call-start = ((), (), s32[]{:S(2)}) async-start(), calls=%async_computation.12 | async-start | bytes 7864320
  418.0 0.7 copy-start.8
  418.1 160.3 %reduce-scatter.23.cloned.1.call-start = ((), (), s32[]{:S(2)}) async-start(), calls=%async_computation.11 | async-start | bytes 7864320
  449.6 191.2 %reduce-scatter.19.cloned.1.call-start = ((), (), s32[]{:S(2)}) async-start(), calls=%async_computation.9 | async-start | bytes 7864320
  469.2 234.0 %reduce-scatter.21.cloned.1.call-start = ((), (), s32[]{:S(2)}) async-start(), calls=%async_computation.10 | async-start | bytes 7864320
  517.2 0.7 copy-start.11
  517.3 248.7 %all-gather.14.cloned.1.call-start = ((), (), s32[]{:S(2)}) async-start(), calls=%async_computation.8 | async-start | bytes 7864320 | tf_op jit(solution)/reshape | solution.py:52
  528.4 302.0 %all-gather.12.cloned.1.call-start = ((), (), s32[]{:S(2)}) async-start(), calls=%async_computation.7 | async-start | bytes 7864320 | tf_op jit(solution)/reshape | solution.py:52
  586.2 308.7 %all-gather.10.cloned.1.call-start = ((), (), s32[]{:S(2)}) async-start(), calls=%async_computation.6 | async-start | bytes 7864320 | tf_op jit(solution)/reshape | solution.py:52
  894.8 6.6 copy-start.1
  894.8 9.8 %slice-start = ((s8[6291456]{0:T(1024)(128)(4,1)}), s8[4194304]{0:T(1024)(128)(4,1)S(1)}, s32[]{:S(2)}) async-start(s8[6291456]{0:T(1024)(128)(4,1)} %bitcast.370), calls=%async_computation.15 | async-start | bytes 8388608
  901.4 4.5 slice-start.1
  (1 other events, 0.6 us)
Sparse Core Ops, SparseCore 0:
  329.4 62.7 reduce-scatter.28
  394.5 59.5 reduce-scatter.26
  457.0 59.5 reduce-scatter.24
  518.8 59.5 reduce-scatter.22
  581.2 59.5 reduce-scatter.18
  643.5 59.5 reduce-scatter.20
  704.7 61.2 all-gather.13
  768.1 62.2 all-gather.11
  832.5 62.2 all-gather.9
where the time goes:
time: 924 us; the launch traced here: 916 us
  matrix products  394 us (43%)
  waiting for transfers between devices  348 us (38%)
  other arithmetic  126 us (14%)
  local copies, waits for them, and re-layouts  31 us (3%)
  between operations  15.1 us (2%)
    reshape x3, waiting for transfers between devices, step(): t.reshape(-1, *t.shape[2:])  184 us
    unnamed x15, waiting for transfers between devices  164 us
    dot_general x5, matrix products, layer(): up = jnp.dot(a, w['w_up'], preferred_element_type=jnp.float32)  141 us
    dot_general x5, matrix products, layer(): gate = jnp.dot(a, w['w_gate'], preferred_element_type=jnp.float32)  134 us
    dot_general x5, matrix products, matmul(): jnp.dot(a, w, preferred_element_type=jnp.float32).astype(jnp.bfloat16)  119 us
    unnamed x5, other arithmetic  95.5 us
    unnamed x37, local copies, waits for them, and re-layouts  30.4 us
  transfers between devices with their start and end apart: 9, of which 6 were waited for; matrix products, arithmetic and copies ran while one was open for 23% of the time, Pallas kernels for 0%

commit v1 on v0

v1 whole, which is shorter than its diff:
```python
import functools

import jax
import jax.numpy as jnp
from jax import lax
from jax.experimental import pallas as pl
from jax.experimental.pallas import tpu as pltpu
from jax.sharding import PartitionSpec as P

F32, BF16 = jnp.float32, jnp.bfloat16
MESH = pl.DeviceIdType.MESH
PIECE = 128
TF = 512
TB = 1024
SUB = 512
VMEM = 60 * 1024 * 1024


def dot(a, b):
    return jnp.dot(a, b, preferred_element_type=F32)


def dot_nt(a, b):
    return lax.dot_general(a, b, (((1,), (1,)), ((), ())), preferred_element_type=F32)


def normed(h):
    wide = h.astype(F32)
    scale = lax.rsqrt(jnp.mean(wide * wide, -1, keepdims=True) + 1e-6)
    return (wide * scale).astype(BF16)


def fwd_kernel(x_ref, dy_ref, wg_ref, wu_ref, wd_ref, h_ref, a_ref, at_ref, dyt_ref):
    x = x_ref[0]
    a = normed(x)
    a_ref[0] = a
    at_ref[0] = a.T
    dyt_ref[...] = dy_ref[0].T
    acc = None
    for c in range(wg_ref.shape[2] // 512):
        cols = pl.ds(c * 512, 512)
        gate = dot(a, wg_ref[0, :, cols])
        up = dot(a, wu_ref[0, :, cols])
        p = (gate * lax.logistic(gate) * up).astype(BF16)
        part = dot(p, wd_ref[0, cols, :])
        acc = part if acc is None else acc + part
    h = x + acc.astype(BF16)
    h_ref[...] = h
    a2 = normed(h)
    a_ref[1] = a2
    at_ref[1] = a2.T


def forward(x, dy, wg, wu, wd):
    _, tokens, d = x.shape
    ff = wg.shape[2]
    tok = pl.BlockSpec((TF, d), lambda t: (t, 0))
    tokt = pl.BlockSpec((d, TF), lambda t: (0, t))
    tok3 = pl.BlockSpec((1, TF, d), lambda t: (0, t, 0))
    both = pl.BlockSpec((2, TF, d), lambda t: (0, t, 0))
    botht = pl.BlockSpec((2, d, TF), lambda t: (0, 0, t))
    wcol = pl.BlockSpec((1, d, ff), lambda t: (0, 0, 0))
    wrow = pl.BlockSpec((1, ff, d), lambda t: (0, 0, 0))
    shape = lambda *s: jax.ShapeDtypeStruct(s, BF16)
    return pl.pallas_call(
        fwd_kernel,
        grid=(tokens // TF,),
        in_specs=[tok3, tok3, wcol, wcol, wrow],
        out_specs=[tok, both, botht, tokt],
        out_shape=[shape(tokens, d), shape(2, tokens, d), shape(2, d, tokens), shape(d, tokens)],
        compiler_params=pltpu.CompilerParams(vmem_limit_bytes=VMEM, dimension_semantics=("arbitrary",)),
        cost_estimate=pl.CostEstimate(flops=6 * tokens * d * ff, bytes_accessed=2 * (8 * tokens * d + 3 * d * ff), transcendentals=tokens * ff),
        name="forward",
    )(x, dy, wg, wu, wd)


def step_of_adamw(w, m, v, g):
    m = 0.9 * m + 0.1 * g
    v = 0.95 * v + 0.05 * g * g
    w = w.astype(F32)
    return (w - 0.02 * (m * lax.rsqrt(v + 1e-8) + 0.1 * w)).astype(BF16)


def bwd_kernel(n, per_layer, *refs):
    refs = list(refs)
    take = lambda k: [refs.pop(0) for _ in range(k)]
    a_ref, at_ref, h_ref = take(3)
    wg_refs, wu_refs, wd_refs = take(n), take(n), take(n)
    dy_hbm, dyt_hbm, wg_hbm, wu_hbm, wd_hbm, mg_hbm, mu_hbm, md_hbm, vg_hbm, vu_hbm, vd_hbm = take(11)
    wag, gs = take(2)
    d_s, dt_s, da_s, wg_s, wu_s, wd_s, accg, accu, accd = take(9)
    grads, far_a, far_b, near_a, near_b, new_s, gst, w_st, m_st, v_st = take(10)
    init_sem, send_sem, recv_sem, st_sem, gs_sem, own_sem = take(6)

    u, t = pl.program_id(0), pl.program_id(1)
    nt = pl.num_programs(1)
    units = 2 * per_layer
    dm, f = accg.shape
    half = PIECE // 2
    share = per_layer * PIECE
    me = lax.axis_index("dp")
    right, left, across = lax.rem(me + 1, n), lax.rem(me + n - 1, n), lax.rem(me + 2, n)

    def remote(kind, par, src, dst, to):
        return pltpu.make_async_remote_copy(
            src_ref=src, dst_ref=dst, send_sem=send_sem.at[kind, par], recv_sem=recv_sem.at[kind, par], device_id={"dp": to}, device_id_type=MESH
        )

    low, high = pl.ds(0, half), pl.ds(half, half)

    def far(par):
        return (
            remote(0, par, grads.at[par, across, :, low, :], far_a.at[par], right),
            remote(1, par, grads.at[par, across, :, high, :], far_b.at[par], left),
        )

    def near(par):
        return (
            remote(2, par, grads.at[par, right], near_a.at[par], right),
            remote(3, par, grads.at[par, left], near_b.at[par], left),
        )

    def out_near(unit, par):
        return (
            remote(4, par, new_s.at[par], wag.at[unit, me], right),
            remote(5, par, new_s.at[par], wag.at[unit, me], left),
        )

    def out_far(unit, par):
        return (
            remote(6, par, wag.at[unit, left, :, low, :], wag.at[unit, left, :, low, :], right),
            remote(7, par, wag.at[unit, right, :, high, :], wag.at[unit, right, :, high, :], left),
        )

    def own_copy(unit, par):
        return pltpu.make_async_copy(new_s.at[par], wag.at[unit, me], own_sem.at[par])

    def gs_copy(unit, par):
        return pltpu.make_async_copy(gst.at[par], gs.at[unit], gs_sem.at[par])

    def stage(unit):
        layer = jnp.where(unit < per_layer, 1, 0)
        at = lax.rem(unit, per_layer) * PIECE
        rows = pl.ds(pl.multiple_of(me * (dm // n), dm // n), dm // n)
        copies = []
        for k, (w, m, v) in enumerate(((wg_hbm, mg_hbm, vg_hbm), (wu_hbm, mu_hbm, vu_hbm))):
            for d in range(n):
                cols = pl.ds(pl.multiple_of(d * share + at, PIECE), PIECE)
                to = pl.ds(d * PIECE, PIECE)
                copies += [(w.at[layer, rows, cols], w_st.at[k, :, to]), (m.at[layer, :, cols], m_st.at[k, :, to]), (v.at[layer, :, cols], v_st.at[k, :, to])]
        own = pl.ds(pl.multiple_of(at, PIECE), PIECE)
        copies += [
            (wd_hbm.at[layer, pl.ds(pl.multiple_of(me * share + at, PIECE), PIECE), :], w_st.at[2]),
            (md_hbm.at[layer, own, :], m_st.at[2]),
            (vd_hbm.at[layer, own, :], v_st.at[2]),
        ]
        return [pltpu.make_async_copy(src, dst, st_sem.at[i]) for i, (src, dst) in enumerate(copies)]

    def slot(i):
        unit, older = u - 1, u - 2
        par, opar = lax.rem(unit + 2, 2), lax.rem(older + 2, 2)
        summing = (unit >= 0) & (unit < units)
        sharing = (older >= 0) & (older < units)
        if i != 0:
            return

        @pl.when((t == 0) & summing)
        def _():
            for copy in far(par):
                copy.start()

        @pl.when((t == 1) & summing)
        def _():
            for copy in far(par):
                copy.wait()
            for to, part, got in ((right, low, far_a), (left, high, far_b)):
                total = grads[par, to, :, part, :].astype(F32) + got[par].astype(F32)
                grads[par, to, :, part, :] = total.astype(BF16)
            for copy in near(par):
                copy.start()
            for copy in stage(unit):
                copy.start()

        @pl.when((t == 1) & sharing)
        def _():
            for copy in out_near(older, opar):
                copy.wait()
            own_copy(older, opar).wait()
            for copy in out_far(older, opar):
                copy.start()

        @pl.when((t == 3) & summing)
        def _():
            for copy in near(par):
                copy.wait()
            for copy in stage(unit):
                copy.wait()

            @pl.when(unit >= 2)
            def _():
                gs_copy(unit - 2, par).wait()

            for k in range(3):
                total = grads[par, me, k].astype(F32) + near_a[par, k].astype(F32) + near_b[par, k].astype(F32)
                total = total.astype(BF16)
                gst[par, k] = total
                new_s[par, k] = step_of_adamw(w_st[k], m_st[k], v_st[k], total.astype(F32))
            for copy in out_near(unit, par):
                copy.start()
            own_copy(unit, par).start()
            gs_copy(unit, par).start()

        @pl.when((t == 3) & sharing)
        def _():
            for copy in out_far(older, opar):
                copy.wait()

        @pl.when((t == 3) & (u == units + 1))
        def _():
            gs_copy(units - 2, 0).wait()
            gs_copy(units - 1, 1).wait()

    def init(k):
        rows = pl.ds(pl.multiple_of(k * TB, TB), TB)
        return (
            pltpu.make_async_copy(dy_hbm.at[0, rows, :], d_s.at[rows, :], init_sem.at[0, k]),
            pltpu.make_async_copy(dyt_hbm.at[:, rows], dt_s.at[:, rows], init_sem.at[1, k]),
        )

    @pl.when((u == 0) & (t == 0))
    def _():
        for k in range(d_s.shape[0] // TB):
            for copy in init(k):
                copy.start()
        barrier = pltpu.get_barrier_semaphore()
        for to in (left, right):
            pl.semaphore_signal(barrier, inc=1, device_id={"dp": to}, device_id_type=MESH)
        pl.semaphore_wait(barrier, 2)

    @pl.when(u == 0)
    def _():
        for copy in init(t):
            copy.wait()

    @pl.when((u < units) & (t == 0))
    def _():
        accg[...] = jnp.zeros_like(accg)
        accu[...] = jnp.zeros_like(accu)
        accd[...] = jnp.zeros_like(accd)
        for k in range(n):
            to = pl.ds(k * PIECE, PIECE)
            wg_s[:, to] = wg_refs[k][0]
            wu_s[:, to] = wu_refs[k][0]
            wd_s[to, :] = wd_refs[k][0]

    here = pl.ds(pl.multiple_of(t * TB, TB), TB)

    @pl.when(u == 0)
    def _():
        da_s[here, :] = jnp.zeros((TB, dm), F32)

    def compute(i, with_da):
        rows = pl.ds(i * SUB, SUB)
        sub = pl.ds(pl.multiple_of(t * TB + i * SUB, SUB), SUB)
        wg, wu, wd = wg_s[...], wu_s[...], wd_s[...]
        a, d = a_ref[0, rows, :], d_s[sub, :]
        gate = dot(a, wg)
        up = dot(a, wu)
        dp = dot_nt(d, wd).astype(BF16).astype(F32)
        s = lax.logistic(gate)
        silu = gate * s
        p = (silu * up).astype(BF16)
        dup = (dp * silu).astype(BF16)
        dgate = (dp * up * (s + silu * (1.0 - s))).astype(BF16)
        at = at_ref[0, :, rows]
        accg[...] += dot(at, dgate)
        accu[...] += dot(at, dup)
        accd[...] += dot(dt_s[:, sub], p)
        if with_da:
            da_s[sub, :] += dot_nt(dgate, wg) + dot_nt(dup, wu)

    slot(0)

    @pl.when(u < per_layer)
    def _():
        for i in range(TB // SUB):
            compute(i, True)

    @pl.when((u >= per_layer) & (u < units))
    def _():
        for i in range(TB // SUB):
            compute(i, False)

    @pl.when((u < units) & (t == nt - 1))
    def _():
        par = lax.rem(u, 2)
        for k in range(n):
            part = pl.ds(k * PIECE, PIECE)
            grads[par, k, 0] = accg[part, :].astype(BF16)
            grads[par, k, 1] = accu[part, :].astype(BF16)
            grads[par, k, 2] = accd[:, part].astype(BF16).T

    @pl.when(u == per_layer - 1)
    def _():
        da = da_s[here, :].astype(BF16).astype(F32)
        wide = h_ref[...].astype(F32)
        scale = lax.rsqrt(jnp.mean(wide * wide, -1, keepdims=True) + 1e-6)
        along = jnp.mean(da * wide, -1, keepdims=True)
        dn = (da * scale - wide * (along * (scale * scale * scale))).astype(BF16)
        dh = d_s[here, :] + dn
        d_s[here, :] = dh
        dt_s[:, here] = dh.T


def backward(n, a, at, h, dy, dyt, wg, wu, wd, moments):
    _, tokens, dm = a.shape
    layers, _, ff = wg.shape
    nt = tokens // TB
    f = n * PIECE
    per_layer = ff // f
    units = layers * per_layer
    now = lambda u: jnp.minimum(u, units - 1)
    layer = lambda u: jnp.where(u < per_layer, 1, 0)
    piece = lambda k: lambda u, t: (layer(u), 0, k * per_layer + lax.rem(now(u), per_layer))
    piece_t = lambda k: lambda u, t: (layer(u), k * per_layer + lax.rem(now(u), per_layer), 0)
    step = lambda u, t: jnp.where(u < units, t, nt - 1)
    hbm = pl.BlockSpec(memory_space=pl.ANY)
    in_specs = [
        pl.BlockSpec((1, TB, dm), lambda u, t: (layer(u), step(u, t), 0)),
        pl.BlockSpec((1, dm, TB), lambda u, t: (layer(u), 0, step(u, t))),
        pl.BlockSpec((TB, dm), lambda u, t: (jnp.where(u == per_layer - 1, t, jnp.where(u < per_layer, 0, nt - 1)), 0)),
        *[pl.BlockSpec((1, dm, PIECE), piece(k)) for k in range(n)] * 1,
        *[pl.BlockSpec((1, dm, PIECE), piece(k)) for k in range(n)],
        *[pl.BlockSpec((1, PIECE, dm), piece_t(k)) for k in range(n)],
        *[hbm] * 11,
    ]
    chunk = (3, PIECE, dm)
    part = (3, PIECE // 2, dm)
    dma = pltpu.SemaphoreType.DMA
    return pl.pallas_call(
        functools.partial(bwd_kernel, n, per_layer),
        grid=(units + 2, nt),
        in_specs=in_specs,
        out_specs=[hbm, hbm],
        out_shape=[jax.ShapeDtypeStruct((units, n, *chunk), BF16), jax.ShapeDtypeStruct((units, *chunk), BF16)],
        scratch_shapes=[
            pltpu.VMEM((tokens, dm), BF16),
            pltpu.VMEM((dm, tokens), BF16),
            pltpu.VMEM((tokens, dm), F32),
            pltpu.VMEM((dm, f), BF16),
            pltpu.VMEM((dm, f), BF16),
            pltpu.VMEM((f, dm), BF16),
            pltpu.VMEM((dm, f), F32),
            pltpu.VMEM((dm, f), F32),
            pltpu.VMEM((dm, f), F32),
            pltpu.VMEM((2, n, *chunk), BF16),
            pltpu.VMEM((2, *part), BF16),
            pltpu.VMEM((2, *part), BF16),
            pltpu.VMEM((2, *chunk), BF16),
            pltpu.VMEM((2, *chunk), BF16),
            pltpu.VMEM((2, *chunk), BF16),
            pltpu.VMEM((2, *chunk), BF16),
            pltpu.VMEM(chunk, BF16),
            pltpu.VMEM(chunk, F32),
            pltpu.VMEM(chunk, F32),
            dma((2, nt)),
            dma((8, 2)),
            dma((8, 2)),
            dma((6 * n + 3,)),
            dma((2,)),
            dma((2,)),
        ],
        compiler_params=pltpu.CompilerParams(
            vmem_limit_bytes=VMEM, dimension_semantics=("arbitrary", "arbitrary"), collective_id=0, has_side_effects=True
        ),
        cost_estimate=pl.CostEstimate(flops=14 * layers * tokens * dm * ff, bytes_accessed=12 * tokens * ff, transcendentals=layers * tokens * ff),
        name="backward",
    )(a, at, h, *[wg] * n, *[wu] * n, *[wd] * n, dy, dyt, wg, wu, wd, *moments)


def finish_kernel(n, per_layer, wag, gs, *refs):
    olds, outs = refs[:6], refs[6:]
    q = pl.program_id(1)
    share = per_layer * PIECE
    rows = outs[3].shape[1]
    lanes = outs[5].shape[2]
    mine = pl.ds(pl.multiple_of(q * rows, rows), rows)
    some = pl.ds(pl.multiple_of(q * lanes, lanes), lanes)

    def moments(k, where, g):
        g = g.astype(F32)
        outs[3 + k][where] = 0.9 * olds[k][where] + 0.1 * g
        outs[6 + k][where] = 0.95 * olds[3 + k][where] + 0.05 * g * g

    for j in range(per_layer):
        down = pl.ds(j * PIECE, PIECE)
        outs[2][0, down, :] = wag[j, 0, 2]
        moments(2, (0, down, slice(None)), gs[j, 2, :, some])
        for d in range(n):
            cols = pl.ds(d * share + j * PIECE, PIECE)
            for k in range(2):
                outs[k][0, :, cols] = wag[j, 0, k, :, d * PIECE : (d + 1) * PIECE]
                moments(k, (0, slice(None), cols), gs[j, k, mine, d * PIECE : (d + 1) * PIECE])


def finish(n, wag, gs, olds):
    units, _, _, _, dm = wag.shape
    layers, rows, ff = olds[0].shape
    per_layer = units // layers
    share = per_layer * PIECE
    small = [pl.BlockSpec((1, rows // n, ff), lambda l, q: (l, q, 0))] * 2 + [pl.BlockSpec((1, share, dm // n), lambda l, q: (l, 0, q))]
    whole = [pl.BlockSpec((1, rows, ff), lambda l, q: (l, q, 0))] * 2 + [pl.BlockSpec((1, share, dm), lambda l, q: (l, q, 0))]
    return pl.pallas_call(
        functools.partial(finish_kernel, n, per_layer),
        grid=(layers, n),
        in_specs=[
            pl.BlockSpec((per_layer, 1, 3, PIECE, dm), lambda l, q: (layers - 1 - l, q, 0, 0, 0)),
            pl.BlockSpec((per_layer, 3, PIECE, dm), lambda l, q: (layers - 1 - l, 0, 0, 0)),
            *small,
            *small,
        ],
        out_specs=[*whole, *small, *small],
        out_shape=[jax.ShapeDtypeStruct((layers, dm, ff), BF16)] * 2
        + [jax.ShapeDtypeStruct((layers, ff, dm), BF16)]
        + [jax.ShapeDtypeStruct(one.shape, F32) for one in olds],
        compiler_params=pltpu.CompilerParams(vmem_limit_bytes=VMEM, dimension_semantics=("arbitrary", "arbitrary")),
        name="finish",
    )(wag, gs, *olds)


def solution(mesh):
    n = mesh.shape["dp"]

    def step(x, dy, wg, wu, wd, *olds):
        h, a, at, dyt = forward(x, dy, wg, wu, wd)
        wag, gs = backward(n, a, at, h, dy, dyt, wg, wu, wd, olds)
        return tuple(finish(n, wag, gs, olds))

    whole = P(None, None, None)
    rows = P(None, "dp", None)
    seq = P(("rep", "dp"), None, None)
    return jax.shard_map(
        step,
        mesh=mesh,
        in_specs=(seq, seq, whole, whole, whole, *[rows] * 6),
        out_specs=(*[P("rep", None, None)] * 3, *[P("rep", "dp", None)] * 6),
        check_vma=False,
    )
```

time: 924 us -> 435 us (0.47)
  Pallas kernels: 0 us -> 434 us
  matrix products: 394 us -> 0 us
  waiting for transfers between devices: 348 us -> 0 us
  other arithmetic: 126 us -> 0 us
  local copies, waits for them, and re-layouts: 31 us -> 0 us
  between operations: 15.1 us -> 0.81 us
    pallas_call x0 -> x3, Pallas kernels: none -> 434 us  [the longest x1 357 us: backward(): pl.pallas_call(functools.partial(bwd_kernel, n, per_layer), grid=(units +...]
    dot_general x15 -> x0, matrix products: 394 us -> none  [the longest x5 141 us: layer(): up = jnp.dot(a, w['w_up'], preferred_element_type=jnp.float32)]
    reshape x3 -> x0, waiting for transfers between devices: 184 us -> none  [step(): t.reshape(-1, *t.shape[2:])]
    unnamed x15 -> x0, waiting for transfers between devices: 164 us -> none
    unnamed x5 -> x0, other arithmetic: 95.5 us -> none
    unnamed x37 -> x0, local copies, waits for them, and re-layouts: 30.4 us -> none
    reshape x3 -> x0, other arithmetic: 18.5 us -> none  [step(): t.reshape(-1, *t.shape[2:])]
  transfers between devices with their start and end apart: 9 -> 0, of which waited for: 6 -> 0; matrix products, arithmetic and copies ran while one was open for 23% -> 0% of each run, Pallas kernels for 0% -> 0%
where the time goes in v1:
time: 435 us
  Pallas kernels  434 us (100%)
    pallas_call x1, Pallas kernels, backward(): pl.pallas_call(functools.partial(bwd_kernel, n, per_layer), grid=(units +...  357 us
    pallas_call x1, Pallas kernels, forward(): pl.pallas_call(fwd_kernel, grid=(tokens // TF,), in_specs=[tok3, tok3, wc...  49.4 us
    pallas_call x1, Pallas kernels, finish(): pl.pallas_call(functools.partial(finish_kernel, n, per_layer), grid=(laye...  27.6 us

profile of v1, /device:TPU:112, one launch (start us, length us, event | category | flops | bytes accessed | tf_op | source)
XLA Modules:
  0.0 435.0 jit_solution(1082824863128645288)
XLA Ops:
  0.6 49.4 %forward.1 = (bf16[4096,512]{1,0:T(8,128)(2,1)}, bf16[2,4096,512]{2,1,0:T(8,128)(2,1)}, bf16[2,512,4096]{2,1,0:T(8,128)(2,1)}, bf16[512,4096]{1,0:T(8,128)(2,1)}) custom-call(bf16[1,4096,512]{2,1,0:T(8,128)(2,1)} %x_ref.1, bf16[1,4096,512]{2,1,0:T(8,128)(2,1)} %refs_15_.1, bf16[2,512,3072]{2,1,0:T(8,128)(2,1)} %refs_17_.1, bf16[2,512,3072]{2,1,0:T(8,128)(2,1)} %refs_18_.1, ...), custom_call_target="tpu_custom_call" | custom-call | flops 38654705664 | bytes 42991616 | tf_op jit(solution)/shard_map/forward/pallas_call | solution.py:65
  50.1 357.1 %backward.1 = (bf16[12,4,3,128,512]{4,3,2,1,0:T(8,128)(2,1)}, bf16[12,3,128,512]{3,2,1,0:T(8,128)(2,1)}) custom-call(bf16[2,4096,512]{2,1,0:T(8,128)(2,1)} %get-tuple-element.15.refs_0_, bf16[2,512,4096]{2,1,0:T(8,128)(2,1)} %get-tuple-element.16.refs_1_, bf16[4096,512]{1,0:T(8,128)(2,1)} %get-tuple-element.17.refs_2_, bf16[2,512,3072]{2,1,0:T(8,128)(2,1)} %refs_17_.1, ...), custom_call_target="tpu_custom_call" | custom-call | flops 180388626432 | bytes 150994944 | tf_op jit(solution)/shard_map/backward/pallas_call | solution.py:340
  407.2 27.6 %finish.1 = (bf16[2,512,3072]{2,1,0:T(8,128)(2,1)}, bf16[2,512,3072]{2,1,0:T(8,128)(2,1)}, bf16[2,3072,512]{2,1,0:T(8,128)(2,1)}, f32[2,128,3072]{2,1,0:T(8,128)...) custom-call(bf16[12,4,3,128,512]{4,3,2,1,0:T(8,128)(2,1)} %get-tuple, ...), custom_call_target="tpu_custom_call" | custom-call | tf_op jit(solution)/shard_map/finish/pallas_call | solution.py:413

commit v2 on v1

--- a/solution.py
+++ b/solution.py
@@ -114,22 +114,34 @@
             remote(1, par, grads.at[par, across, :, high, :], far_b.at[par], left),
         )
 
-    def near(par):
-        return (
-            remote(2, par, grads.at[par, right], near_a.at[par], right),
-            remote(3, par, grads.at[par, left], near_b.at[par], left),
-        )
-
-    def out_near(unit, par):
-        return (
-            remote(4, par, new_s.at[par], wag.at[unit, me], right),
-            remote(5, par, new_s.at[par], wag.at[unit, me], left),
+    def plain(par):
+        return (
+            remote(2, par, grads.at[par, right, :, high, :], near_a.at[par, :, high, :], right),
+            remote(3, par, grads.at[par, left, :, low, :], near_b.at[par, :, low, :], left),
+        )
+
+    def joined(par):
+        return (
+            remote(4, par, grads.at[par, right, :, low, :], near_a.at[par, :, low, :], right),
+            remote(5, par, grads.at[par, left, :, high, :], near_b.at[par, :, high, :], left),
+        )
+
+    def out_first(unit, par):
+        return (
+            remote(6, par, new_s.at[par, :, low, :], wag.at[unit, me, :, low, :], right),
+            remote(7, par, new_s.at[par, :, high, :], wag.at[unit, me, :, high, :], left),
+        )
+
+    def out_second(unit, par):
+        return (
+            remote(8, par, new_s.at[par, :, high, :], wag.at[unit, me, :, high, :], right),
+            remote(9, par, new_s.at[par, :, low, :], wag.at[unit, me, :, low, :], left),
         )
 
     def out_far(unit, par):
         return (
-            remote(6, par, wag.at[unit, left, :, low, :], wag.at[unit, left, :, low, :], right),
-            remote(7, par, wag.at[unit, right, :, high, :], wag.at[unit, right, :, high, :], left),
+            remote(10, par, wag.at[unit, left, :, low, :], wag.at[unit, left, :, low, :], right),
+            remote(11, par, wag.at[unit, right, :, high, :], wag.at[unit, right, :, high, :], left),
         )
 
     def own_copy(unit, par):
@@ -156,42 +168,44 @@
         ]
         return [pltpu.make_async_copy(src, dst, st_sem.at[i]) for i, (src, dst) in enumerate(copies)]
 
-    def slot(i):
-        unit, older = u - 1, u - 2
+    def exchange():
+        unit, older, oldest = u - 1, u - 2, u - 3
         par, opar = lax.rem(unit + 2, 2), lax.rem(older + 2, 2)
         summing = (unit >= 0) & (unit < units)
         sharing = (older >= 0) & (older < units)
-        if i != 0:
-            return
 
         @pl.when((t == 0) & summing)
         def _():
-            for copy in far(par):
-                copy.start()
-
-        @pl.when((t == 1) & summing)
+            for copy in far(par) + plain(par):
+                copy.start()
+
+        @pl.when((t == 2) & (oldest >= 0))
+        def _():
+            for copy in out_far(oldest, par):
+                copy.wait()
+
+        @pl.when((t == 2) & summing)
         def _():
             for copy in far(par):
                 copy.wait()
             for to, part, got in ((right, low, far_a), (left, high, far_b)):
                 total = grads[par, to, :, part, :].astype(F32) + got[par].astype(F32)
                 grads[par, to, :, part, :] = total.astype(BF16)
-            for copy in near(par):
+            for copy in joined(par):
                 copy.start()
             for copy in stage(unit):
                 copy.start()
 
-        @pl.when((t == 1) & sharing)
-        def _():
-            for copy in out_near(older, opar):
-                copy.wait()
-            own_copy(older, opar).wait()
+        @pl.when((t == 2) & sharing)
+        def _():
+            for copy in out_first(older, opar):
+                copy.wait()
             for copy in out_far(older, opar):
                 copy.start()
 
         @pl.when((t == 3) & summing)
         def _():
-            for copy in near(par):
+            for copy in plain(par) + joined(par):
                 copy.wait()
             for copy in stage(unit):
                 copy.wait()
@@ -205,18 +219,21 @@
                 total = total.astype(BF16)
                 gst[par, k] = total
                 new_s[par, k] = step_of_adamw(w_st[k], m_st[k], v_st[k], total.astype(F32))
-            for copy in out_near(unit, par):
+            for copy in out_first(unit, par) + out_second(unit, par):
                 copy.start()
             own_copy(unit, par).start()
             gs_copy(unit, par).start()
 
         @pl.when((t == 3) & sharing)
         def _():
-            for copy in out_far(older, opar):
-                copy.wait()
+            for copy in out_second(older, opar):
+                copy.wait()
+            own_copy(older, opar).wait()
 
         @pl.when((t == 3) & (u == units + 1))
         def _():
+            for copy in out_far(units - 1, 1):
+                copy.wait()
             gs_copy(units - 2, 0).wait()
             gs_copy(units - 1, 1).wait()
 
@@ -279,7 +296,7 @@
         if with_da:
             da_s[sub, :] += dot_nt(dgate, wg) + dot_nt(dup, wu)
 
-    slot(0)
+    exchange()
 
     @pl.when(u < per_layer)
     def _():
@@ -364,8 +381,8 @@
             pltpu.VMEM(chunk, F32),
             pltpu.VMEM(chunk, F32),
             dma((2, nt)),
-            dma((8, 2)),
-            dma((8, 2)),
+            dma((12, 2)),
+            dma((12, 2)),
             dma((6 * n + 3,)),
             dma((2,)),
             dma((2,)),

time: 435 us -> 419 us (0.963)
  Pallas kernels: 434 us -> 418 us
    pallas_call x1, Pallas kernels: 357 us -> 341 us  [backward(): pl.pallas_call(functools.partial(bwd_kernel, n, per_layer), grid=(units +...]
where the time goes in v2:
time: 419 us
  Pallas kernels  418 us (100%)
    pallas_call x1, Pallas kernels, backward(): pl.pallas_call(functools.partial(bwd_kernel, n, per_layer), grid=(units +...  341 us
    pallas_call x1, Pallas kernels, forward(): pl.pallas_call(fwd_kernel, grid=(tokens // TF,), in_specs=[tok3, tok3, wc...  49.4 us
    pallas_call x1, Pallas kernels, finish(): pl.pallas_call(functools.partial(finish_kernel, n, per_layer), grid=(laye...  27.6 us

profile of v2, /device:TPU:112, one launch (start us, length us, event | category | flops | bytes accessed | tf_op | source)
XLA Modules:
  0.0 419.1 jit_solution(14839013203243342711)
XLA Ops:
  0.6 49.4 %forward.1 = (bf16[4096,512]{1,0:T(8,128)(2,1)}, bf16[2,4096,512]{2,1,0:T(8,128)(2,1)}, bf16[2,512,4096]{2,1,0:T(8,128)(2,1)}, bf16[512,4096]{1,0:T(8,128)(2,1)}) custom-call(bf16[1,4096,512]{2,1,0:T(8,128)(2,1)} %x_ref.1, bf16[1,4096,512]{2,1,0:T(8,128)(2,1)} %refs_15_.1, bf16[2,512,3072]{2,1,0:T(8,128)(2,1)} %refs_17_.1, bf16[2,512,3072]{2,1,0:T(8,128)(2,1)} %refs_18_.1, ...), custom_call_target="tpu_custom_call" | custom-call | flops 38654705664 | bytes 42991616 | tf_op jit(solution)/shard_map/forward/pallas_call | solution.py:65
  50.1 341.2 %backward.1 = (bf16[12,4,3,128,512]{4,3,2,1,0:T(8,128)(2,1)}, bf16[12,3,128,512]{3,2,1,0:T(8,128)(2,1)}) custom-call(bf16[2,4096,512]{2,1,0:T(8,128)(2,1)} %get-tuple-element.15.refs_0_, bf16[2,512,4096]{2,1,0:T(8,128)(2,1)} %get-tuple-element.16.refs_1_, bf16[4096,512]{1,0:T(8,128)(2,1)} %get-tuple-element.17.refs_2_, bf16[2,512,3072]{2,1,0:T(8,128)(2,1)} %refs_17_.1, ...), custom_call_target="tpu_custom_call" | custom-call | flops 180388626432 | bytes 150994944 | tf_op jit(solution)/shard_map/backward/pallas_call | solution.py:357
  391.3 27.6 %finish.1 = (bf16[2,512,3072]{2,1,0:T(8,128)(2,1)}, bf16[2,512,3072]{2,1,0:T(8,128)(2,1)}, bf16[2,3072,512]{2,1,0:T(8,128)(2,1)}, f32[2,128,3072]{2,1,0:T(8,128)...) custom-call(bf16[12,4,3,128,512]{4,3,2,1,0:T(8,128)(2,1)} %get-tuple, ...), custom_call_target="tpu_custom_call" | custom-call | tf_op jit(solution)/shard_map/finish/pallas_call | solution.py:430
